TPU v7x, 512 devices: a whole 4x8x8 slice. The times are simulated.
512 devices in a mesh: dp: 64 (over z_hi, y, core), mp: 8 (over x, z_lo).
Axes of the slice: x: 4, y: 8, z: 8 (z_hi: 4, z_lo: 2; z = z_hi * 2 + z_lo), core: 2. Of those that a mesh axis runs over, the one named last changes fastest.
Arguments:
- features: bfloat16 [3072, 384], P('dp'), may hold values from -100 to 100
- teacher_weight: float32 [384, 131072], P(None, ('dp', 'mp')), may hold values from -250 to 250
- student_weight: float32 [384, 131072], P(None, ('dp', 'mp')), may hold values from -24 to 24
- center: float32 [131072], P(('dp', 'mp')), may hold values from -1 to 1
Outputs:
- blended: float32 [384, 131072], P(None, ('dp', 'mp'))
- new_center: float32 [131072], P(('dp', 'mp'))
- log_targets: float32 [3072, 131072], P(None, ('dp', 'mp'))
All inputs are finite; a program needn't handle non-finite values.
Results may differ from a plain program's by a relative error of at most 0.0003.
Values may be sent and summed in bfloat16 or wider, within the bound.
A program may use at most 64 MiB of HBM per device.

v0:
```python
import jax
import jax.numpy as jnp
from jax import lax
from jax.sharding import PartitionSpec as P

ema_momentum = 0.994
center_momentum = 0.9
teacher_temp = 0.07
epsilon = 1e-06


def copy_for_each(array, axis):
    length = lax.axis_size(axis)
    return lax.all_to_all(
        jnp.broadcast_to(array[None], (length, *array.shape)), axis, 0, 0, tiled=True
    )


def laid_out(tiles, dim):
    tiles = jnp.moveaxis(tiles, 0, dim)
    shape = tiles.shape
    return tiles.reshape(*shape[:dim], shape[dim] * shape[dim + 1], *shape[dim + 2 :])


def gathered_copies(array, axis, dim):
    tiles = copy_for_each(array, axis)
    return laid_out(tiles, dim)


def over_copies(array, axis):
    everything = copy_for_each(array, axis)
    return jnp.sum(everything, axis=0)


def shards(features, teacher_weight, student_weight, center):
    blended = ema_momentum * teacher_weight + (1.0 - ema_momentum) * student_weight
    col_norm = jnp.sqrt(jnp.sum(blended * blended, axis=0, keepdims=True) + epsilon)
    protos = (blended / col_norm).astype(jnp.bfloat16)
    wide_feats = features.astype(jnp.float32)
    row_norm = jnp.sqrt(jnp.sum(wide_feats * wide_feats, axis=1, keepdims=True) + epsilon)
    unit_rows = (wide_feats / row_norm).astype(jnp.bfloat16)
    images = features.shape[0] * lax.axis_size("dp")
    groups = lax.axis_size("mp")
    dp_count = lax.axis_size("dp")
    member = lax.axis_index("mp")
    rows_each = features.shape[0] // groups
    block_width = protos.shape[1]
    own_rows = lax.dynamic_slice_in_dim(unit_rows, member * rows_each, rows_each, 0)
    gathered = gathered_copies(own_rows, "dp", 0)
    block_logits = jnp.dot(
        gathered, gathered_copies(protos, "mp", 1), preferred_element_type=jnp.float32
    )
    placed_center = lax.dynamic_update_slice_in_dim(
        jnp.zeros((block_logits.shape[1],), jnp.float32),
        center_momentum * center,
        member * block_width,
        0,
    )
    contribution = placed_center + (1.0 - center_momentum) * (
        jnp.sum(block_logits, axis=0) / images
    )
    block_center = over_copies(contribution, "mp")
    new_center = lax.dynamic_slice_in_dim(block_center, member * block_width, block_width, 0)
    shifted = (block_logits - block_center[None, :]) / teacher_temp
    totals = over_copies(jnp.sum(jnp.exp(shifted), axis=1), "dp")
    normed = shifted - jnp.log(totals)[:, None]
    arrived = lax.all_to_all(
        normed.reshape(dp_count, rows_each, groups, block_width),
        "mp",
        split_axis=2,
        concat_axis=1,
        tiled=True,
    )
    log_targets = arrived.reshape(dp_count * groups * rows_each, block_width)
    return (blended, new_center, log_targets)


def solution(mesh):
    placed = (P("dp", None), P(None, ("dp", "mp")), P(None, ("dp", "mp")), P(("dp", "mp")))
    return jax.shard_map(
        shards,
        mesh=mesh,
        in_specs=placed,
        out_specs=(P(None, ("dp", "mp")), P(("dp", "mp")), P(None, ("dp", "mp"))),
        check_vma=False,
    )
```

profile of v0, /device:TPU:1, one launch (start us, length us, event | category | flops | bytes accessed | tf_op | source)
XLA Modules:
  0.0 152.9 jit_solution(13815081778427370517)
XLA Ops:
  0.6 0.9 multiply_reduce_fusion.1
  1.5 0.8 convert_element_type.9
  2.5 0.8 broadcast_in_dim.8
  3.3 17.6 %all-to-all-start = ((bf16[64,6,384]{2,1,0:T(8,128)(2,1)}), bf16[64,6,384]{2,1,0:T(8,128)(2,1)S(1)}, u32[]{:S(2)}, u32[]{:S(2)}) async-start(bf16[64,6,384]{2,1,0:T(8,128)(2,1)} %broadcast_in_dim.8), calls=%async_computation | async-start | bytes 786432 | tf_op jit(solution)/shard_map/all_to_all | solution.py:14
  20.9 1.2 multiply_reduce_fusion
  22.1 0.2 copy.16
  22.3 14.6 %all-to-all-done = bf16[64,6,384]{2,1,0:T(8,128)(2,1)S(1)} async-done(((bf16[64,6,384]{2,1,0:T(8,128)(2,1)}), bf16[64,6,384]{2,1,0:T(8,128)(2,1)S(1)}, u32[]{:S(2)}, u32[]{:S(2)}) %all-to-all-start) | async-done | bytes 294944 | tf_op jit(solution)/shard_map/all_to_all | solution.py:14
  36.9 1.3 broadcast_in_dim.9
  38.2 4.6 %all-to-all-start.1 = ((bf16[8,384,256]{1,2,0:T(8,128)(2,1)}), bf16[8,384,256]{1,2,0:T(8,128)(2,1)S(1)}, u32[]{:S(2)}, u32[]{:S(2)}) async-start(bf16[8,384,256]{1,2,0:T(8,128)(2,1)} %broadcast_in_dim.9), calls=%async_computation.1 | async-start | bytes 3145728 | tf_op jit(solution)/shard_map/all_to_all | solution.py:14
  43.0 20.1 %all-to-all-done.1 = bf16[8,384,256]{1,2,0:T(8,128)(2,1)S(1)} async-done(((bf16[8,384,256]{1,2,0:T(8,128)(2,1)}), bf16[8,384,256]{1,2,0:T(8,128)(2,1)S(1)}, u32[]{:S(2)}, u32[]{:S(2)}) %all-to-all-start.1) | async-done | bytes 1572896 | tf_op jit(solution)/shard_map/all_to_all | solution.py:14
  63.0 1.1 copy-done
  64.2 2.4 %fusion.2 = (f32[2048]{0:T(1024)S(1)}, f32[384,2048]{1,0:T(8,128)S(1)}) fusion(bf16[384,384]{1,0:T(8,128)(2,1)S(1)} %reshape.64, bf16[384,2048]{0,1:T(8,128)(2,1)} %bitcast.16), kind=kOutput, calls=%fused_computation.13 | convolution fusion | flops 604764160 | bytes 5021696 | tf_op jit(solution)/shard_map/dot_general | solution.py:50
  66.6 0.2 add_dynamic-update-slice_fusion
  66.9 9.0 %all_to_all.37 = f32[8,1,2048]{2,1,0:T(1,128)S(1)} all-to-all(f32[8,1,2048]{2,1,0:T(1,128)S(1)} %broadcast_in_dim.10), channel_id=1, replica_groups=mesh['dp'=64,'mp'=8] {'mp'}, dimensions={0} | all-to-all | bytes 131072 | tf_op jit(solution)/shard_map/all_to_all | solution.py:14
  76.0 0.6 exponential_reduce_fusion
  76.6 20.9 %all_to_all.38 = f32[64,1,384]{2,1,0:T(1,128)S(1)} all-to-all(f32[64,1,384]{2,1,0:T(1,128)S(1)} %broadcast_in_dim.11), channel_id=1, replica_groups=mesh['dp'=64,'mp'=8] {'dp'}, dimensions={0} | all-to-all | bytes 196608 | tf_op jit(solution)/shard_map/all_to_all | solution.py:14
  97.6 0.4 fusion
  98.0 1.4 copy.23
  99.4 3.5 %copy.19 = f32[64,6,8,256]{3,0,1,2:T(8,128)} copy(f32[64,6,8,256]{3,2,1,0:T(8,128)S(1)} %bitcast.15) | data formatting | bytes 6291456 | tf_op jit(solution)/shard_map/reshape | solution.py:68
  102.9 3.7 %all-to-all-start.4 = ((f32[64,6,8,256]{3,0,1,2:T(8,128)}), f32[64,6,8,256]{3,0,1,2:T(8,128)S(1)}, u32[]{:S(2)}, u32[]{:S(2)}) async-start(f32[64,6,8,256]{3,0,1,2:T(8,128)} %copy.19), calls=%async_computation.4 | async-start | bytes 6291456 | tf_op jit(solution)/shard_map/all_to_all | solution.py:67
  106.6 0.6 dynamic_slice.7
  107.2 37.2 %all-to-all-done.4 = f32[64,6,8,256]{3,0,1,2:T(8,128)S(1)} async-done(((f32[64,6,8,256]{3,0,1,2:T(8,128)}), f32[64,6,8,256]{3,0,1,2:T(8,128)S(1)}, u32[]{:S(2)}, u32[]{:S(2)}) %all-to-all-start.4) | async-done | bytes 3145760 | tf_op jit(solution)/shard_map/all_to_all | solution.py:67
  144.4 3.8 %copy.20 = f32[64,8,6,1,256]{4,2,1,0,3:T(8,128)} copy(f32[64,8,6,1,256]{4,0,2,1,3:T(8,128)S(1)} %bitcast.13) | data formatting | bytes 6291456 | tf_op jit(solution)/shard_map/all_to_all | solution.py:67
  148.3 4.6 %reshape.67 = f32[3072,256]{1,0:T(8,128)} reshape(f32[64,8,6,1,256]{4,2,1,0,3:T(8,128)} %copy.20) | data formatting | bytes 6291456 | tf_op jit(solution)/shard_map/reshape | solution.py:74
  (17 shorter events, 0.6 us)
Async XLA Ops:
  3.3 33.7 %all-to-all-start = ((bf16[64,6,384]{2,1,0:T(8,128)(2,1)}), bf16[64,6,384]{2,1,0:T(8,128)(2,1)S(1)}, u32[]{:S(2)}, u32[]{:S(2)}) async-start(bf16[64,6,384]{2,1,0:T(8,128)(2,1)} %broadcast_in_dim.8), calls=%async_computation | async-start | bytes 786432 | tf_op jit(solution)/shard_map/all_to_all | solution.py:14
  22.1 20.9 %copy-start.1 = (f32[384,256]{1,0:T(8,128)}, f32[384,256]{1,0:T(8,128)S(1)}, u32[]{:S(2)}) copy-start(f32[384,256]{1,0:T(8,128)S(1)} %get-tuple-element.4) | copy-start | bytes 1179652
  38.2 24.8 %all-to-all-start.1 = ((bf16[8,384,256]{1,2,0:T(8,128)(2,1)}), bf16[8,384,256]{1,2,0:T(8,128)(2,1)S(1)}, u32[]{:S(2)}, u32[]{:S(2)}) async-start(bf16[8,384,256]{1,2,0:T(8,128)(2,1)} %broadcast_in_dim.9), calls=%async_computation.1 | async-start | bytes 3145728 | tf_op jit(solution)/shard_map/all_to_all | solution.py:14
  42.8 23.8 %copy-start.2 = (f32[256]{0:T(256)S(1)}, f32[256]{0:T(256)}, u32[]{:S(2)}) copy-start(f32[256]{0:T(256)} %param.7) | copy-start | bytes 3076
  63.0 1.1 copy-start
  102.9 41.5 %all-to-all-start.4 = ((f32[64,6,8,256]{3,0,1,2:T(8,128)}), f32[64,6,8,256]{3,0,1,2:T(8,128)S(1)}, u32[]{:S(2)}, u32[]{:S(2)}) async-start(f32[64,6,8,256]{3,0,1,2:T(8,128)} %copy.19), calls=%async_computation.4 | async-start | bytes 6291456 | tf_op jit(solution)/shard_map/all_to_all | solution.py:67
where the time goes:
time: 154 us; the launch traced here: 153 us
  waiting for transfers between devices  71.9 us (47%)
  blocking collectives  29.9 us (19%)
  starting transfers between devices  25.9 us (17%)
  local copies, waits for them, and re-layouts  17.6 us (11%)
  other arithmetic  4.32 us (3%)
  matrix products  2.42 us (2%)
    all_to_all x1, waiting for transfers between devices, shards(): lax.all_to_all(normed.reshape(dp_count, rows_each, groups, block_width),...  37.2 us
    all_to_all x2, waiting for transfers between devices, copy_for_each(): lax.all_to_all(jnp.broadcast_to(array[None], (length, *array.shape)), axi...  34.7 us
    all_to_all x2, blocking collectives, copy_for_each(): lax.all_to_all(jnp.broadcast_to(array[None], (length, *array.shape)), axi...  29.9 us
    all_to_all x2, starting transfers between devices, copy_for_each(): lax.all_to_all(jnp.broadcast_to(array[None], (length, *array.shape)), axi...  22.2 us
    reshape x1, local copies, waits for them, and re-layouts, shards(): log_targets = arrived.reshape(dp_count * groups * rows_each, block_width)  4.62 us
    all_to_all x1, local copies, waits for them, and re-layouts, shards(): lax.all_to_all(normed.reshape(dp_count, rows_each, groups, block_width),...  3.81 us
    all_to_all x1, starting transfers between devices, shards(): lax.all_to_all(normed.reshape(dp_count, rows_each, groups, block_width),...  3.65 us
    reshape x1, local copies, waits for them, and re-layouts, shards(): normed.reshape(dp_count, rows_each, groups, block_width)  3.49 us
  transfers between devices with their start and end apart: 3, of which 3 were waited for; matrix products, arithmetic and copies ran while one was open for 1% of the time, Pallas kernels for 0%

commit v1 on v0

v1 whole, which is shorter than its diff:
```python
import jax
import jax.numpy as jnp
from jax import lax
from jax.experimental import pallas as pl
from jax.experimental.pallas import tpu as pltpu
from jax.sharding import PartitionSpec as P

ema_momentum = 0.994
center_momentum = 0.9
teacher_temp = 0.07
epsilon = 1e-06

MESH = pl.DeviceIdType.MESH
NX, NY, NZ, NH = 4, 8, 8, 4
ROLES = 2 * NX
STEPS = (0, 1, 7, 2, 6, 3, 5, 4)


def gather_kernel(
    feat_ref, tw_ref, sw_ref, center_ref,
    scaled_ref, logs_ref, center_out_ref, blended_ref,
    rows, protos, part, role_buf, y_buf, z_buf, log_buf,
    recv_sem, z_send, y_send, x_send, relay_send, pair_send,
    role_recv, role_send, yb_recv, yb_send, zb_recv, zb_send, log_recv, log_send,
):
    dp = lax.axis_index("dp")
    mp = lax.axis_index("mp")
    core = lax.rem(dp, 2)
    y = lax.rem(lax.div(dp, 2), NY)
    zh = lax.div(dp, 2 * NY)
    x = lax.div(mp, 2)
    zl = lax.rem(mp, 2)
    z = zh * 2 + zl
    images = rows.shape[0] * rows.shape[1] * rows.shape[2] * rows.shape[3]

    def at(x_, y_, z_, c_):
        return ((lax.div(z_, 2) * NY + y_) * 2 + c_, x_ * 2 + lax.rem(z_, 2))

    def xs(k):
        return lax.rem(x + k, NX)

    def ys(k):
        return lax.rem(y + k, NY)

    def zs(k):
        return lax.rem(z + k, NZ)

    role = x * 2 + core

    def role_at(k):
        r = lax.rem(role + k, ROLES)
        return r, at(lax.div(r, 2), y, z, lax.rem(r, 2))

    barrier = pltpu.get_barrier_semaphore()
    for k in range(1, ROLES):
        pl.semaphore_signal(barrier, inc=1, device_id=role_at(k)[1], device_id_type=MESH)
    for k in range(1, NY):
        pl.semaphore_signal(barrier, inc=1, device_id=at(x, ys(k), z, core), device_id_type=MESH)
    for k in range(1, NZ):
        pl.semaphore_signal(barrier, inc=1, device_id=at(x, y, zs(k), core), device_id_type=MESH)

    source = zh == x

    @pl.when(source)
    def _():
        wide = feat_ref[...].astype(jnp.float32)
        norm = jnp.sqrt(jnp.sum(wide * wide, axis=1, keepdims=True) + epsilon)
        rows[x, y, core] = (wide / norm).astype(jnp.bfloat16)

    pl.semaphore_wait(barrier, ROLES + NY + NZ - 3)

    pending = []

    def send(slot, send_sem, target):
        copy = pltpu.make_async_remote_copy(
            src_ref=rows.at[slot],
            dst_ref=rows.at[slot],
            send_sem=send_sem,
            recv_sem=recv_sem.at[slot],
            device_id=target,
            device_id_type=MESH,
        )
        copy.start()
        pending.append(copy)

    def arrive(slot):
        pltpu.make_async_remote_copy(
            src_ref=rows.at[slot],
            dst_ref=rows.at[slot],
            send_sem=z_send.at[0],
            recv_sem=recv_sem.at[slot],
            device_id=at(x, y, z, 1 - core),
            device_id_type=MESH,
        ).wait_recv()

    def z_copy(k):
        slot = (x, y, core)
        step = jnp.where(zl == 1, k, NZ - k)
        return pltpu.make_async_remote_copy(
            src_ref=rows.at[slot],
            dst_ref=rows.at[slot],
            send_sem=z_send.at[k - 1],
            recv_sem=recv_sem.at[slot],
            device_id=at(x, y, zs(step), core),
            device_id_type=MESH,
        )

    @pl.when(source)
    def _():
        for k in range(1, 4):
            z_copy(k).start()

    blended = ema_momentum * tw_ref[...] + (1.0 - ema_momentum) * sw_ref[...]
    blended_ref[...] = blended
    col_norm = jnp.sqrt(jnp.sum(blended * blended, axis=0, keepdims=True) + epsilon)
    protos[...] = (blended / col_norm).astype(jnp.bfloat16)

    pair_count = [0]

    def to_pair(slot):
        send(slot, pair_send.at[pair_count[0]], at(x, y, z, 1 - core))
        pair_count[0] += 1

    def own_stage(i):
        slot = (x, ys(STEPS[i]), core)
        if i == 0:
            @pl.when(jnp.logical_not(source))
            def _():
                arrive(slot)

            for k in range(1, NY):
                send(slot, y_send.at[k - 1], at(x, ys(STEPS[k]), z, core))
        else:
            arrive(slot)
        send(slot, x_send.at[0, i], at(xs(1), y, z, core))
        send(slot, x_send.at[1, i], at(xs(NX - 1), y, z, core))
        to_pair(slot)

    def near_stage(i):
        yy = ys(STEPS[i])
        for k in (NX - 1, 1):
            slot = (xs(k), yy, core)
            arrive(slot)
            if (i % 2 == 0) == (k == 1):
                send(slot, relay_send.at[i], at(xs(NX - k), y, z, core))
            to_pair(slot)

    def far_stage(i):
        slot = (xs(2), ys(STEPS[i]), core)
        arrive(slot)
        to_pair(slot)

    for i in range(NY + 3):
        if i < NY:
            own_stage(i)
        if 1 <= i < NY + 1:
            near_stage(i - 1)
        if 3 <= i:
            far_stage(i - 3)

    sums = jnp.zeros((1, protos.shape[1]), jnp.float32)
    block = rows.shape[1] * rows.shape[2] * rows.shape[3]
    for k in (0, 1, 3, 2):
        group = xs(k)
        for i in range(NY):
            arrive((group, ys(STEPS[i]), 1 - core))
        lhs = rows[group].reshape(block, rows.shape[4])
        logits = jnp.dot(lhs, protos[...], preferred_element_type=jnp.float32)
        sums = sums + jnp.sum(logits, axis=0, keepdims=True)
        scaled_ref[group] = logits * (1.0 / teacher_temp)

    new_center = center_momentum * center_ref[...] + (1.0 - center_momentum) * (sums / images)
    center_out_ref[...] = new_center
    shift = new_center * (1.0 / teacher_temp)

    half = protos.shape[1] // 2
    each = images // ROLES
    ones = jnp.ones((8, 2 * half), jnp.bfloat16)
    for j in range(ROLES):
        group, start = j // 2, (j % 2) * each
        e = jnp.exp(scaled_ref[group, start:start + each, :] - shift)
        folded = e[:, :half] + e[:, half:]
        high = folded.astype(jnp.bfloat16)
        low = (folded - high.astype(jnp.float32)).astype(jnp.bfloat16)
        both = jnp.concatenate([high, low], axis=1)
        total = lax.dot_general(
            ones, both, (((1,), (1,)), ((), ())), preferred_element_type=jnp.float32
        )
        part[j] = total[0:1]

    def exchange(src, src_slot, dst, dst_slot, ssem, rsem, target):
        copy = pltpu.make_async_remote_copy(
            src_ref=src.at[src_slot],
            dst_ref=dst.at[dst_slot],
            send_sem=ssem,
            recv_sem=rsem,
            device_id=target,
            device_id_type=MESH,
        )
        copy.start()
        pending.append(copy)

    def landed(dst, slot, rsem, ssem):
        pltpu.make_async_remote_copy(
            src_ref=dst.at[slot],
            dst_ref=dst.at[slot],
            send_sem=ssem,
            recv_sem=rsem,
            device_id=at(x, y, z, 1 - core),
            device_id_type=MESH,
        ).wait_recv()

    for k in range(1, ROLES):
        r, target = role_at(k)
        exchange(part, r, role_buf, role, role_send.at[k - 1], role_recv.at[role], target)
    role_buf[role] = part[role]
    for k in range(1, ROLES):
        r, _ = role_at(k)
        landed(role_buf, r, role_recv.at[r], role_send.at[0])
    y_buf[y] = jnp.sum(role_buf[...], axis=0)

    for k in range(1, NY):
        exchange(y_buf, y, y_buf, y, yb_send.at[k - 1], yb_recv.at[y], at(x, ys(k), z, core))
    for k in range(1, NY):
        landed(y_buf, ys(k), yb_recv.at[ys(k)], yb_send.at[0])
    z_buf[z] = jnp.sum(y_buf[...], axis=0)

    for k in range(1, NZ):
        exchange(z_buf, z, z_buf, z, zb_send.at[k - 1], zb_recv.at[z], at(x, y, zs(k), core))
    for k in range(1, NZ):
        landed(z_buf, zs(k), zb_recv.at[zs(k)], zb_send.at[0])
    log_buf[role] = jnp.log(jnp.sum(z_buf[...], axis=0))

    for k in range(1, ROLES):
        _, target = role_at(k)
        exchange(log_buf, role, log_buf, role, log_send.at[k - 1], log_recv.at[role], target)
    for k in range(1, ROLES):
        r, _ = role_at(k)
        landed(log_buf, r, log_recv.at[r], log_send.at[0])
    logs_ref[...] = log_buf[...]

    @pl.when(source)
    def _():
        for k in range(1, 4):
            z_copy(k).wait_send()

    for copy in pending:
        copy.wait_send()


def write_kernel(scaled_ref, logs_ref, center_ref, blended_ref, out_ref, blended_out, center_out, stage, sem):
    early = (
        pltpu.make_async_copy(blended_ref, blended_out, sem.at[ROLES]),
        pltpu.make_async_copy(center_ref, center_out, sem.at[ROLES + 1]),
    )
    for copy in early:
        copy.start()
    shift = center_ref[...] * (1.0 / teacher_temp)
    each = stage.shape[1]
    copies = []
    for j in range(ROLES):
        group, start = j // 2, (j % 2) * each
        for i in range(each // 128):
            row = logs_ref[j, :, i * 128:(i + 1) * 128]
            column = jnp.broadcast_to(row, (128, 128)).T
            both = jnp.concatenate([column, column], axis=1)
            there = slice(start + i * 128, start + (i + 1) * 128)
            stage[j, i * 128:(i + 1) * 128, :] = (scaled_ref[group, there, :] - shift) - both
        copy = pltpu.make_async_copy(stage.at[j], out_ref.at[pl.ds(j * each, each)], sem.at[j])
        copy.start()
        copies.append(copy)
    for copy in copies:
        copy.wait()
    for copy in early:
        copy.wait()


def shards(features, teacher_weight, student_weight, center):
    rows_here, depth = features.shape
    width = teacher_weight.shape[1]
    images = rows_here * lax.axis_size("dp")
    each = images // ROLES
    vmem = pl.BlockSpec(memory_space=pltpu.VMEM)
    anywhere = pl.BlockSpec(memory_space=pl.ANY)
    f32 = jnp.float32
    dma = pltpu.SemaphoreType.DMA
    small = lambda n: pltpu.VMEM((n, 1, each), f32)
    scaled, logs, new_center, blended = pl.pallas_call(
        gather_kernel,
        out_shape=(
            jax.ShapeDtypeStruct((NH, images // NH, width), f32),
            jax.ShapeDtypeStruct((ROLES, 1, each), f32),
            jax.ShapeDtypeStruct((1, width), f32),
            jax.ShapeDtypeStruct((depth, width), f32),
        ),
        in_specs=[vmem] * 4,
        out_specs=[vmem] * 4,
        scratch_shapes=[
            pltpu.VMEM((NH, NY, 2, rows_here, depth), jnp.bfloat16),
            pltpu.VMEM((depth, width), jnp.bfloat16),
            small(ROLES), small(ROLES), small(NY), small(NZ), small(ROLES),
            dma((NH, NY, 2)), dma((3,)), dma((NY - 1,)), dma((2, NY)), dma((NY,)), dma((NH * NY,)),
            dma((ROLES,)), dma((ROLES - 1,)), dma((NY,)), dma((NY - 1,)),
            dma((NZ,)), dma((NZ - 1,)), dma((ROLES,)), dma((ROLES - 1,)),
        ],
        compiler_params=pltpu.CompilerParams(collective_id=0, has_side_effects=True),
        name="gather",
    )(features, teacher_weight, student_weight, center.reshape(1, width))
    log_targets, blended, new_center = pl.pallas_call(
        write_kernel,
        out_shape=(
            jax.ShapeDtypeStruct((images, width), f32),
            jax.ShapeDtypeStruct((depth, width), f32),
            jax.ShapeDtypeStruct((1, width), f32),
        ),
        in_specs=[vmem] * 4,
        out_specs=[anywhere] * 3,
        scratch_shapes=[pltpu.VMEM((ROLES, each, width), f32), dma((ROLES + 2,))],
        name="write",
    )(scaled, logs, new_center, blended)
    return (blended, new_center.reshape(width), log_targets)


def solution(mesh):
    placed = (P("dp", None), P(None, ("dp", "mp")), P(None, ("dp", "mp")), P(("dp", "mp")))
    return jax.shard_map(
        shards,
        mesh=mesh,
        in_specs=placed,
        out_specs=(P(None, ("dp", "mp")), P(("dp", "mp")), P(None, ("dp", "mp"))),
        check_vma=False,
    )
```

time: 154 us -> 69.5 us (0.45)
  waiting for transfers between devices: 71.9 us -> 0 us
  Pallas kernels: 0 us -> 68.7 us
  blocking collectives: 29.9 us -> 0 us
  starting transfers between devices: 25.9 us -> 0 us
  local copies, waits for them, and re-layouts: 17.6 us -> 0 us
  other arithmetic: 4.32 us -> 0 us
  matrix products: 2.42 us -> 0 us
    all_to_all x3 -> x0, waiting for transfers between devices: 71.9 us -> none  [the longest x1 37.2 us: shards(): lax.all_to_all(normed.reshape(dp_count, rows_each, groups, block_width),...]
    pallas_call x0 -> x2, Pallas kernels: none -> 68.7 us  [the longest x1 64.9 us: shards(): pl.pallas_call(gather_kernel, out_shape=(jax.ShapeDtypeStruct((NH, images...]
    all_to_all x2 -> x0, blocking collectives: 29.9 us -> none  [copy_for_each(): lax.all_to_all(jnp.broadcast_to(array[None], (length, *array.shape)), axi...]
    all_to_all x3 -> x0, starting transfers between devices: 25.9 us -> none  [the longest x2 22.2 us: copy_for_each(): lax.all_to_all(jnp.broadcast_to(array[None], (length, *array.shape)), axi...]
    reshape x3 -> x0, local copies, waits for them, and re-layouts: 8.21 us -> none  [the longest x1 4.62 us: shards(): log_targets = arrived.reshape(dp_count * groups * rows_each, block_width)]
    all_to_all x1 -> x0, local copies, waits for them, and re-layouts: 3.81 us -> none  [shards(): lax.all_to_all(normed.reshape(dp_count, rows_each, groups, block_width),...]
    reduce_sum x5 -> x0, other arithmetic: 2.84 us -> none  [the longest x1 1.22 us: shards(): jnp.sum(blended * blended, axis=0, keepdims=True) + epsilon]
    unnamed x7 -> x0, local copies, waits for them, and re-layouts: 2.57 us -> none
  transfers between devices with their start and end apart: 3 -> 0, of which waited for: 3 -> 0; matrix products, arithmetic and copies ran while one was open for 1% -> 0% of each run, Pallas kernels for 0% -> 0%
where the time goes in v1:
time: 69.5 us; the launch traced here: 69.3 us
  Pallas kernels  68.7 us (99%)
    pallas_call x1, Pallas kernels, shards(): pl.pallas_call(gather_kernel, out_shape=(jax.ShapeDtypeStruct((NH, images...  64.9 us
    pallas_call x1, Pallas kernels, shards(): pl.pallas_call(write_kernel, out_shape=(jax.ShapeDtypeStruct((images, wid...  3.84 us

profile of v1, /device:TPU:1, one launch (start us, length us, event | category | flops | bytes accessed | tf_op | source)
XLA Modules:
  0.0 69.3 jit_solution(4100296082488966266)
XLA Ops:
  0.6 64.9 %gather.1 = (f32[4,768,256]{2,1,0:T(8,128)}, f32[8,1,384]{2,1,0:T(1,128)}, f32[1,256]{1,0:T(1,128)}, f32[384,256]{1,0:T(8,128)}) custom-call(bf16[48,384]{1,0:T(8,128)(2,1)} %feat_ref.1, f32[384,256]{1,0:T(8,128)} %tw_ref.1, f32[384,256]{1,0:T(8,128)} %sw_ref.1, f32[1,256]{1,0:T(1,128)} %bitcast.2), custom_call_target="tpu_custom_call" | custom-call | tf_op jit(solution)/shard_map/gather/pallas_call | solution.py:288
  65.5 3.8 %write.1 = (f32[3072,256]{1,0:T(8,128)}, f32[384,256]{1,0:T(8,128)}, f32[1,256]{1,0:T(1,128)}) custom-call(f32[4,768,256]{2,1,0:T(8,128)} %get-tuple-element.10.scaled_ref, f32[8,1,384]{2,1,0:T(1,128)} %get-tuple-element.11.logs_ref, f32[1,256]{1,0:T(1,128)} %get-tuple-element.12.center_ref, f32[384,256]{1,0:T(8,128)} %get-tuple-element.13.blended_ref), custom_call_target="tpu_custom_call" | custom-call | tf_op jit(solution)/shard_map/write/pallas_call | solution.py:309

commit v2 on v1

v2 whole, which is shorter than its diff:
```python
import jax
import jax.numpy as jnp
from jax import lax
from jax.experimental import pallas as pl
from jax.experimental.pallas import tpu as pltpu
from jax.sharding import PartitionSpec as P

ema_momentum = 0.994
center_momentum = 0.9
teacher_temp = 0.07
epsilon = 1e-06

MESH = pl.DeviceIdType.MESH
NX, NY, NZ, NH = 4, 8, 8, 4
ROLES = 2 * NX
STEPS = (0, 1, 7, 2, 6, 3, 5, 4)


def gather_kernel(
    feat_hbm, tw_hbm, sw_hbm, center_hbm,
    scaled_ref, logs_ref, center_out_ref, blended_ref,
    feat, student, center, rows, protos, part, role_buf, y_buf, z_buf, log_buf,
    load_sem, recv_sem, z_send, y_send, cross_send, pair_send,
    role_recv, role_send, yb_recv, yb_send, zb_recv, zb_send, log_recv, log_send,
):
    dp = lax.axis_index("dp")
    mp = lax.axis_index("mp")
    core = lax.rem(dp, 2)
    y = lax.rem(lax.div(dp, 2), NY)
    zh = lax.div(dp, 2 * NY)
    x = lax.div(mp, 2)
    zl = lax.rem(mp, 2)
    z = zh * 2 + zl
    images = rows.shape[0] * rows.shape[1] * rows.shape[2] * rows.shape[3]

    def at(x_, y_, z_, c_):
        return ((lax.div(z_, 2) * NY + y_) * 2 + c_, x_ * 2 + lax.rem(z_, 2))

    def xs(k):
        return lax.rem(x + k, NX)

    def ys(k):
        return lax.rem(y + k, NY)

    def zs(k):
        return lax.rem(z + k, NZ)

    role = x * 2 + core

    def role_at(k):
        r = lax.rem(role + k, ROLES)
        return r, at(lax.div(r, 2), y, z, lax.rem(r, 2))

    pair = at(x, y, z, 1 - core)

    barrier = pltpu.get_barrier_semaphore()
    for k in range(1, NZ):
        pl.semaphore_signal(barrier, inc=1, device_id=at(x, y, zs(k), core), device_id_type=MESH)
    for k in range(1, NY):
        pl.semaphore_signal(barrier, inc=1, device_id=at(x, ys(k), z, core), device_id_type=MESH)
    for k in range(1, ROLES):
        pl.semaphore_signal(barrier, inc=1, device_id=role_at(k)[1], device_id_type=MESH)

    loads = [
        pltpu.make_async_copy(feat_hbm, feat, load_sem.at[0]),
        pltpu.make_async_copy(tw_hbm, blended_ref, load_sem.at[1]),
        pltpu.make_async_copy(sw_hbm, student, load_sem.at[2]),
        pltpu.make_async_copy(center_hbm, center, load_sem.at[3]),
    ]
    for load in loads:
        load.start()

    spread_x = core == 1
    base = jnp.where(spread_x, x, zh)
    source = jnp.logical_or(core == 0, zh == x)
    fetched = jnp.logical_and(core == 1, zh == x)
    sign = jnp.where(zl == 1, 1, NZ - 1)

    loads[0].wait()

    @pl.when(source)
    def _():
        wide = feat[...].astype(jnp.float32)
        norm = jnp.sqrt(jnp.sum(wide * wide, axis=1, keepdims=True) + epsilon)
        rows[base, y, core] = (wide / norm).astype(jnp.bfloat16)

    with jax.named_scope("barrier"):
        pl.semaphore_wait(barrier, ROLES + NY + NZ - 3)

    pending = []

    def block_copy(slot, send_sem, target):
        return pltpu.make_async_remote_copy(
            src_ref=rows.at[slot],
            dst_ref=rows.at[slot],
            send_sem=send_sem,
            recv_sem=recv_sem.at[slot],
            device_id=target,
            device_id_type=MESH,
        )

    def send(slot, send_sem, target):
        copy = block_copy(slot, send_sem, target)
        copy.start()
        pending.append(copy)

    def arrive(slot):
        block_copy(slot, z_send.at[0], pair).wait_recv()

    def z_target(k):
        return zs(lax.rem(sign * k, NZ))

    def z_copy(k):
        return block_copy((base, y, core), z_send.at[k - 1], at(x, y, z_target(k), core))

    @pl.when(fetched)
    def _():
        for k in range(1, NH):
            z_copy(k).start()

    pair_count = [0]

    def to_pair(slot):
        send(slot, pair_send.at[pair_count[0]], pair)
        pair_count[0] += 1

    def spread(slot, i):
        for n, k in enumerate((1, 3, 2)):
            k_z = n + 1
            target = at(
                jnp.where(spread_x, xs(k), x), y, jnp.where(spread_x, z, z_target(k_z)), core
            )
            send(slot, cross_send.at[n, i], target)
        to_pair(slot)

    def own_stage(i):
        slot = (base, ys(STEPS[i]), core)
        if i == 0:
            @pl.when(jnp.logical_not(source))
            def _():
                arrive(slot)

            for k in range(1, NY):
                send(slot, y_send.at[k - 1], at(x, ys(STEPS[k]), z, core))
        else:
            arrive(slot)
        spread(slot, i)

    def cross_stage(i):
        for k in (1, 3, 2):
            slot = (lax.rem(base + k, NH), ys(STEPS[i]), core)
            arrive(slot)
            to_pair(slot)

    with jax.named_scope("own0"):
        own_stage(0)

    loads[1].wait()
    loads[2].wait()
    blended = ema_momentum * blended_ref[...] + (1.0 - ema_momentum) * student[...]
    blended_ref[...] = blended
    col_norm = jnp.sqrt(jnp.sum(blended * blended, axis=0, keepdims=True) + epsilon)
    protos[...] = (blended / col_norm).astype(jnp.bfloat16)

    for i in range(1, NY):
        with jax.named_scope(f"own{i}"):
            own_stage(i)

    sums = [jnp.zeros((1, protos.shape[1]), jnp.float32)]

    def dot_stage(i):
        yy = ys(STEPS[i])
        with jax.named_scope(f"pair{i}"):
            for group in range(NH):
                arrive((group, yy, 1 - core))
        lhs = rows[:, yy].reshape(NH * 2 * rows.shape[3], rows.shape[4])
        logits = jnp.dot(lhs, protos[...], preferred_element_type=jnp.float32)
        sums[0] = sums[0] + jnp.sum(logits, axis=0, keepdims=True)
        scaled = logits * (1.0 / teacher_temp)
        scaled_ref[:, yy] = scaled.reshape(NH, 2 * rows.shape[3], protos.shape[1])

    for i in range(NY):
        with jax.named_scope(f"cross{i}"):
            cross_stage(i)
        if i >= 1:
            dot_stage(i - 1)
    dot_stage(NY - 1)

    loads[3].wait()
    new_center = center_momentum * center[...] + (1.0 - center_momentum) * (sums[0] / images)
    center_out_ref[...] = new_center
    shift = new_center * (1.0 / teacher_temp)

    half = protos.shape[1] // 2
    pieces = 4
    each = images // (2 * pieces)
    ones = jnp.ones((8, 2 * half), jnp.bfloat16)
    for j in range(2 * pieces):
        group, start = j // 2, (j % 2) * (NY // 2)
        e = jnp.exp(scaled_ref[group, start:start + NY // 2] - shift).reshape(each, 2 * half)
        folded = e[:, :half] + e[:, half:]
        high = folded.astype(jnp.bfloat16)
        low = (folded - high.astype(jnp.float32)).astype(jnp.bfloat16)
        both = jnp.concatenate([high, low], axis=1)
        total = lax.dot_general(
            ones, both, (((1,), (1,)), ((), ())), preferred_element_type=jnp.float32
        )
        where = (j % pieces) * each
        part[j // pieces, :, where:where + each] = total[0:1]

    def exchange(src, src_slot, dst, dst_slot, ssem, rsem, target):
        copy = pltpu.make_async_remote_copy(
            src_ref=src.at[src_slot],
            dst_ref=dst.at[dst_slot],
            send_sem=ssem,
            recv_sem=rsem,
            device_id=target,
            device_id_type=MESH,
        )
        copy.start()
        pending.append(copy)

    def landed(dst, slot, rsem, ssem):
        pltpu.make_async_remote_copy(
            src_ref=dst.at[slot],
            dst_ref=dst.at[slot],
            send_sem=ssem,
            recv_sem=rsem,
            device_id=pair,
            device_id_type=MESH,
        ).wait_recv()

    with jax.named_scope("role"):
        for k in range(1, ROLES):
            r, target = role_at(k)
            exchange(
                part, lax.rem(r, 2), role_buf, role, role_send.at[k - 1], role_recv.at[role], target
            )
        role_buf[role] = part[core]
        for k in range(1, ROLES):
            r, _ = role_at(k)
            landed(role_buf, r, role_recv.at[r], role_send.at[0])
        y_buf[y] = jnp.sum(role_buf[...], axis=0)

    with jax.named_scope("ysum"):
        for k in range(1, NY):
            exchange(y_buf, y, y_buf, y, yb_send.at[k - 1], yb_recv.at[y], at(x, ys(k), z, core))
        for k in range(1, NY):
            landed(y_buf, ys(k), yb_recv.at[ys(k)], yb_send.at[0])
        z_buf[z] = jnp.sum(y_buf[...], axis=0)

    with jax.named_scope("zsum"):
        for k in range(1, NZ):
            exchange(z_buf, z, z_buf, z, zb_send.at[k - 1], zb_recv.at[z], at(x, y, zs(k), core))
        for k in range(1, NZ):
            landed(z_buf, zs(k), zb_recv.at[zs(k)], zb_send.at[0])
        log_buf[core] = jnp.log(jnp.sum(z_buf[...], axis=0))

    with jax.named_scope("log"):
        exchange(log_buf, core, log_buf, core, log_send.at[0], log_recv.at[core], pair)
        landed(log_buf, 1 - core, log_recv.at[1 - core], log_send.at[0])
        logs_ref[...] = log_buf[...]

    with jax.named_scope("drain"):
        @pl.when(fetched)
        def _():
            for k in range(1, NH):
                z_copy(k).wait_send()

        for copy in pending:
            copy.wait_send()


def write_kernel(scaled_ref, logs_ref, center_ref, blended_ref, out_ref, blended_out, center_out, stage, sem):
    pieces = stage.shape[0]
    early = (
        pltpu.make_async_copy(blended_ref, blended_out, sem.at[pieces]),
        pltpu.make_async_copy(center_ref, center_out, sem.at[pieces + 1]),
    )
    for copy in early:
        copy.start()
    shift = center_ref[...] * (1.0 / teacher_temp)
    each, width = stage.shape[1:]
    copies = []
    for j in range(pieces):
        group, start = j // 2, (j % 2) * (NY // 2)
        scaled = scaled_ref[group, start:start + NY // 2].reshape(each, width)
        where = (j % (pieces // 2)) * each
        for i in range(each // 128):
            row = logs_ref[j // (pieces // 2), :, where + i * 128:where + (i + 1) * 128]
            column = jnp.broadcast_to(row, (128, 128)).T
            both = jnp.concatenate([column, column], axis=1)
            there = slice(i * 128, (i + 1) * 128)
            stage[j, there, :] = (scaled[there, :] - shift) - both
        copy = pltpu.make_async_copy(stage.at[j], out_ref.at[pl.ds(j * each, each)], sem.at[j])
        copy.start()
        copies.append(copy)
    for copy in copies:
        copy.wait()
    for copy in early:
        copy.wait()


def shards(features, teacher_weight, student_weight, center):
    rows_here, depth = features.shape
    width = teacher_weight.shape[1]
    images = rows_here * lax.axis_size("dp")
    vmem = pl.BlockSpec(memory_space=pltpu.VMEM)
    anywhere = pl.BlockSpec(memory_space=pl.ANY)
    f32 = jnp.float32
    dma = pltpu.SemaphoreType.DMA
    halves = lambda n: pltpu.VMEM((n, 1, images // 2), f32)
    results = pl.pallas_call(
        gather_kernel,
        out_shape=(
            pltpu.VMEM((NH, NY, 2 * rows_here, width), f32),
            halves(2),
            pltpu.VMEM((1, width), f32),
            pltpu.VMEM((depth, width), f32),
        ),
        in_specs=[anywhere] * 4,
        out_specs=[vmem] * 4,
        scratch_shapes=[
            pltpu.VMEM((rows_here, depth), jnp.bfloat16),
            pltpu.VMEM((depth, width), f32),
            pltpu.VMEM((1, width), f32),
            pltpu.VMEM((NH, NY, 2, rows_here, depth), jnp.bfloat16),
            pltpu.VMEM((depth, width), jnp.bfloat16),
            halves(2), halves(ROLES), halves(NY), halves(NZ), halves(2),
            dma((4,)), dma((NH, NY, 2)), dma((NH - 1,)), dma((NY - 1,)), dma((3, NY)), dma((NH * NY,)),
            dma((ROLES,)), dma((ROLES - 1,)), dma((NY,)), dma((NY - 1,)),
            dma((NZ,)), dma((NZ - 1,)), dma((2,)), dma((1,)),
        ],
        compiler_params=pltpu.CompilerParams(collective_id=0, has_side_effects=True),
        name="gather",
    )(features, teacher_weight, student_weight, center.reshape(1, width))
    results = [pltpu.with_memory_space_constraint(r, pltpu.VMEM) for r in results]
    pieces = 8
    log_targets, blended, new_center = pl.pallas_call(
        write_kernel,
        out_shape=(
            jax.ShapeDtypeStruct((images, width), f32),
            jax.ShapeDtypeStruct((depth, width), f32),
            jax.ShapeDtypeStruct((1, width), f32),
        ),
        in_specs=[vmem] * 4,
        out_specs=[anywhere] * 3,
        scratch_shapes=[pltpu.VMEM((pieces, images // pieces, width), f32), dma((pieces + 2,))],
        name="write",
    )(*results)
    return (blended, new_center.reshape(width), log_targets)


def solution(mesh):
    placed = (P("dp", None), P(None, ("dp", "mp")), P(None, ("dp", "mp")), P(("dp", "mp")))
    return jax.shard_map(
        shards,
        mesh=mesh,
        in_specs=placed,
        out_specs=(P(None, ("dp", "mp")), P(("dp", "mp")), P(None, ("dp", "mp"))),
        check_vma=False,
    )
```

time: 69.5 us -> 53.6 us (0.77)
  Pallas kernels: 68.7 us -> 52.8 us
    pallas_call x1, Pallas kernels: 64.9 us -> 50.9 us  [shards(): pl.pallas_call(gather_kernel, out_shape=(pltpu.VMEM((NH, NY, 2 * rows_her...]
    pallas_call x1, Pallas kernels: 3.84 us -> 1.88 us  [shards(): pl.pallas_call(write_kernel, out_shape=(jax.ShapeDtypeStruct((images, wid...]
where the time goes in v2:
time: 53.6 us; the launch traced here: 53.4 us
  Pallas kernels  52.8 us (99%)
  between operations  0.64 us (1%)
    pallas_call x1, Pallas kernels, shards(): pl.pallas_call(gather_kernel, out_shape=(pltpu.VMEM((NH, NY, 2 * rows_her...  50.9 us
    pallas_call x1, Pallas kernels, shards(): pl.pallas_call(write_kernel, out_shape=(jax.ShapeDtypeStruct((images, wid...  1.88 us

profile of v2, /device:TPU:1, one launch (start us, length us, event | category | flops | bytes accessed | tf_op | source)
XLA Modules:
  0.0 53.4 jit_solution(12903594768656703733)
XLA Ops:
  0.6 50.9 %gather.1 = (f32[4,8,96,256]{3,2,1,0:T(8,128)S(1)}, f32[2,1,1536]{2,1,0:T(1,128)S(1)}, f32[1,256]{1,0:T(1,128)S(1)}, f32[384,256]{1,0:T(8,128)S(1)}) custom-call(bf16[48,384]{1,0:T(8,128)(2,1)} %feat_hbm.1, f32[384,256]{1,0:T(8,128)} %tw_hbm.1, f32[384,256]{1,0:T(8,128)} %sw_hbm.1, f32[1,256]{1,0:T(1,128)} %bitcast.2), custom_call_target="tpu_custom_call" | custom-call | tf_op jit(solution)/shard_map/gather/pallas_call | solution.py:313
  51.6 1.9 %write.1 = (f32[3072,256]{1,0:T(8,128)}, f32[384,256]{1,0:T(8,128)}, f32[1,256]{1,0:T(1,128)}) custom-call(f32[4,8,96,256]{3,2,1,0:T(8,128)S(1)} %get-tuple-element.10.scaled_ref, f32[2,1,1536]{2,1,0:T(1,128)S(1)} %get-tuple-element.11.logs_ref, f32[1,256]{1,0:T(1,128)S(1)} %get-tuple-element.12.center_ref, f32[384,256]{1,0:T(8,128)S(1)} %get-tuple-element.13.blended_ref), custom_call_target="tpu_custom_call" | custom-call | tf_op jit(solution)/shard_map/write/pallas_call | solution.py:339

commit v3 on v2

--- a/solution.py
+++ b/solution.py
@@ -20,8 +20,8 @@
     feat_hbm, tw_hbm, sw_hbm, center_hbm,
     scaled_ref, logs_ref, center_out_ref, blended_ref,
     feat, student, center, rows, protos, part, role_buf, y_buf, z_buf, log_buf,
-    load_sem, recv_sem, z_send, y_send, cross_send, pair_send,
-    role_recv, role_send, yb_recv, yb_send, zb_recv, zb_send, log_recv, log_send,
+    load_sem, known_sem, own_recv, near_recv, rest_recv, pair_recv,
+    z_send, y_send, cross_send, pair_send, sum_recv, sum_send,
 ):
     dp = lax.axis_index("dp")
     mp = lax.axis_index("mp")
@@ -53,13 +53,13 @@
 
     pair = at(x, y, z, 1 - core)
 
+    twice = [at(x, ys(2), z, core), at(x, ys(NY - 2), z, core), at(x, y, zs(2), core), at(x, y, zs(NZ - 2), core)]
+    close = [at(x, ys(1), z, core), at(x, ys(NY - 1), z, core), at(x, y, zs(1), core), at(x, y, zs(NZ - 1), core)]
+    close += [pair] + twice + [at(xs(k), y, z, core) for k in range(1, NX)]
+
     barrier = pltpu.get_barrier_semaphore()
-    for k in range(1, NZ):
-        pl.semaphore_signal(barrier, inc=1, device_id=at(x, y, zs(k), core), device_id_type=MESH)
-    for k in range(1, NY):
-        pl.semaphore_signal(barrier, inc=1, device_id=at(x, ys(k), z, core), device_id_type=MESH)
-    for k in range(1, ROLES):
-        pl.semaphore_signal(barrier, inc=1, device_id=role_at(k)[1], device_id_type=MESH)
+    for peer in close:
+        pl.semaphore_signal(barrier, inc=1, device_id=peer, device_id_type=MESH)
 
     loads = [
         pltpu.make_async_copy(feat_hbm, feat, load_sem.at[0]),
@@ -74,9 +74,12 @@
     base = jnp.where(spread_x, x, zh)
     source = jnp.logical_or(core == 0, zh == x)
     fetched = jnp.logical_and(core == 1, zh == x)
+    ahead = lax.rem(zh - x + NH, NH)
+    passed_on = jnp.logical_and(core == 1, ahead == jnp.where(zl == 1, 1, NH - 1))
     sign = jnp.where(zl == 1, 1, NZ - 1)
 
-    loads[0].wait()
+    with jax.named_scope("load"):
+        loads[0].wait()
 
     @pl.when(source)
     def _():
@@ -85,72 +88,105 @@
         rows[base, y, core] = (wide / norm).astype(jnp.bfloat16)
 
     with jax.named_scope("barrier"):
-        pl.semaphore_wait(barrier, ROLES + NY + NZ - 3)
-
-    pending = []
-
-    def block_copy(slot, send_sem, target):
+        pl.semaphore_wait(barrier, len(close))
+    for peer in twice + [pair]:
+        pl.semaphore_signal(known_sem, inc=1, device_id=peer, device_id_type=MESH)
+
+    def block_copy(slot, send_sem, recv_sem, target):
         return pltpu.make_async_remote_copy(
             src_ref=rows.at[slot],
             dst_ref=rows.at[slot],
             send_sem=send_sem,
-            recv_sem=recv_sem.at[slot],
+            recv_sem=recv_sem,
             device_id=target,
             device_id_type=MESH,
         )
 
-    def send(slot, send_sem, target):
-        copy = block_copy(slot, send_sem, target)
-        copy.start()
-        pending.append(copy)
-
-    def arrive(slot):
-        block_copy(slot, z_send.at[0], pair).wait_recv()
+    def sized(blocks, sem):
+        return pltpu.make_async_remote_copy(
+            src_ref=blocks, dst_ref=blocks, send_sem=sem, recv_sem=sem, device_id=pair, device_id_type=MESH
+        )
+
+    def one_block():
+        return rows.at[base, y, core]
 
     def z_target(k):
         return zs(lax.rem(sign * k, NZ))
 
     def z_copy(k):
-        return block_copy((base, y, core), z_send.at[k - 1], at(x, y, z_target(k), core))
+        return block_copy((base, y, core), z_send, own_recv.at[y], at(x, y, z_target(k), core))
 
     @pl.when(fetched)
     def _():
-        for k in range(1, NH):
+        for k in (1, 2):
             z_copy(k).start()
 
-    pair_count = [0]
-
     def to_pair(slot):
-        send(slot, pair_send.at[pair_count[0]], pair)
-        pair_count[0] += 1
-
-    def spread(slot, i):
-        for n, k in enumerate((1, 3, 2)):
-            k_z = n + 1
-            target = at(
-                jnp.where(spread_x, xs(k), x), y, jnp.where(spread_x, z, z_target(k_z)), core
-            )
-            send(slot, cross_send.at[n, i], target)
-        to_pair(slot)
+        block_copy(slot, pair_send, pair_recv.at[slot[1]], pair).start()
+
+    def y_copy(slot, k):
+        block_copy(slot, y_send, own_recv.at[slot[1]], at(x, ys(k), z, core)).start()
+
+    def x_copy(slot, k, sem):
+        block_copy(slot, cross_send, sem.at[slot[1]], at(xs(k), y, z, core)).start()
 
     def own_stage(i):
-        slot = (base, ys(STEPS[i]), core)
+        step = STEPS[i]
+        yy = ys(step)
+        slot = (base, yy, core)
         if i == 0:
             @pl.when(jnp.logical_not(source))
             def _():
-                arrive(slot)
-
-            for k in range(1, NY):
-                send(slot, y_send.at[k - 1], at(x, ys(STEPS[k]), z, core))
+                sized(one_block(), own_recv.at[yy]).wait_recv()
+
+            @pl.when(passed_on)
+            def _():
+                z_copy(1).start()
+
+            for k in (1, NY - 1, 2, NY - 2):
+                y_copy(slot, k)
         else:
-            arrive(slot)
-        spread(slot, i)
-
-    def cross_stage(i):
-        for k in (1, 3, 2):
-            slot = (lax.rem(base + k, NH), ys(STEPS[i]), core)
-            arrive(slot)
-            to_pair(slot)
+            sized(one_block(), own_recv.at[yy]).wait_recv()
+        if step == 2:
+            y_copy(slot, NY - 1)
+        if step == NY - 2:
+            y_copy(slot, 1)
+            back = jnp.where(spread_x, 2, NY - 2)
+            y_copy((base, ys(back), core), NY - back)
+
+        @pl.when(spread_x)
+        def _():
+            x_copy(slot, NX - 1, near_recv)
+            x_copy(slot, 1, rest_recv)
+            x_copy(slot, 2, rest_recv)
+
+        @pl.when(jnp.logical_not(spread_x))
+        def _():
+            block_copy(slot, cross_send, near_recv.at[yy], at(x, y, z_target(1), core)).start()
+
+        to_pair(slot)
+
+    turns = (jnp.where(spread_x, 1, jnp.where(zl == 1, 1, 3)), jnp.where(spread_x, 3, jnp.where(zl == 1, 3, 1)), 2)
+
+    def cross_slot(i, n):
+        return (lax.rem(base + turns[n], NH), ys(STEPS[i]), core)
+
+    def near_stage(i):
+        slot = cross_slot(i, 0)
+        sized(one_block(), near_recv.at[slot[1]]).wait_recv()
+
+        @pl.when(jnp.logical_not(spread_x))
+        def _():
+            for k in (NZ - 1, NZ - 2):
+                block_copy(slot, cross_send, rest_recv.at[slot[1]], at(x, y, z_target(k), core)).start()
+
+        to_pair(slot)
+
+    def rest_stage(i):
+        yy = ys(STEPS[i])
+        sized(rows.at[pl.ds(0, 2), yy, core], rest_recv.at[yy]).wait_recv()
+        for n in (1, 2):
+            to_pair(cross_slot(i, n))
 
     with jax.named_scope("own0"):
         own_stage(0)
@@ -162,29 +198,28 @@
     col_norm = jnp.sqrt(jnp.sum(blended * blended, axis=0, keepdims=True) + epsilon)
     protos[...] = (blended / col_norm).astype(jnp.bfloat16)
 
-    for i in range(1, NY):
-        with jax.named_scope(f"own{i}"):
-            own_stage(i)
-
     sums = [jnp.zeros((1, protos.shape[1]), jnp.float32)]
 
     def dot_stage(i):
         yy = ys(STEPS[i])
-        with jax.named_scope(f"pair{i}"):
-            for group in range(NH):
-                arrive((group, yy, 1 - core))
+        sized(rows.at[:, yy, 1 - core], pair_recv.at[yy]).wait_recv()
         lhs = rows[:, yy].reshape(NH * 2 * rows.shape[3], rows.shape[4])
         logits = jnp.dot(lhs, protos[...], preferred_element_type=jnp.float32)
         sums[0] = sums[0] + jnp.sum(logits, axis=0, keepdims=True)
         scaled = logits * (1.0 / teacher_temp)
         scaled_ref[:, yy] = scaled.reshape(NH, 2 * rows.shape[3], protos.shape[1])
 
-    for i in range(NY):
-        with jax.named_scope(f"cross{i}"):
-            cross_stage(i)
-        if i >= 1:
-            dot_stage(i - 1)
-    dot_stage(NY - 1)
+    stages = {"own": own_stage, "near": near_stage, "rest": rest_stage, "dot": dot_stage}
+    order = (
+        ("own", (1, 2)), ("near", (0,)), ("own", (3, 4)), ("near", (1, 2)), ("rest", (0,)), ("own", (5, 6)),
+        ("near", (3, 4)), ("own", (7,)), ("near", (5, 6)), ("rest", (1, 2)), ("dot", (0,)), ("near", (7,)),
+        ("rest", (3, 4)), ("dot", (1, 2)), ("rest", (5, 6)), ("dot", (3, 4)),
+        ("rest", (7,)), ("dot", (5, 6, 7)),
+    )
+    for name, steps in order:
+        for i in steps:
+            with jax.named_scope(f"{name}{i}"):
+                stages[name](i)
 
     loads[3].wait()
     new_center = center_momentum * center[...] + (1.0 - center_momentum) * (sums[0] / images)
@@ -208,67 +243,54 @@
         where = (j % pieces) * each
         part[j // pieces, :, where:where + each] = total[0:1]
 
-    def exchange(src, src_slot, dst, dst_slot, ssem, rsem, target):
-        copy = pltpu.make_async_remote_copy(
-            src_ref=src.at[src_slot],
-            dst_ref=dst.at[dst_slot],
-            send_sem=ssem,
-            recv_sem=rsem,
-            device_id=target,
-            device_id_type=MESH,
-        )
-        copy.start()
-        pending.append(copy)
-
-    def landed(dst, slot, rsem, ssem):
+    def exchange(src, dst, ssem, rsem, target):
         pltpu.make_async_remote_copy(
-            src_ref=dst.at[slot],
-            dst_ref=dst.at[slot],
-            send_sem=ssem,
-            recv_sem=rsem,
-            device_id=pair,
-            device_id_type=MESH,
-        ).wait_recv()
-
+            src_ref=src, dst_ref=dst, send_sem=ssem, recv_sem=rsem, device_id=target, device_id_type=MESH
+        ).start()
+
+    with jax.named_scope("known"):
+        pl.semaphore_wait(known_sem, len(twice) + 1)
     with jax.named_scope("role"):
         for k in range(1, ROLES):
             r, target = role_at(k)
-            exchange(
-                part, lax.rem(r, 2), role_buf, role, role_send.at[k - 1], role_recv.at[role], target
-            )
+            exchange(part.at[lax.rem(r, 2)], role_buf.at[role], sum_send.at[0], sum_recv.at[0], target)
         role_buf[role] = part[core]
-        for k in range(1, ROLES):
-            r, _ = role_at(k)
-            landed(role_buf, r, role_recv.at[r], role_send.at[0])
+        sized(role_buf.at[pl.ds(0, ROLES - 1)], sum_recv.at[0]).wait_recv()
         y_buf[y] = jnp.sum(role_buf[...], axis=0)
 
     with jax.named_scope("ysum"):
         for k in range(1, NY):
-            exchange(y_buf, y, y_buf, y, yb_send.at[k - 1], yb_recv.at[y], at(x, ys(k), z, core))
-        for k in range(1, NY):
-            landed(y_buf, ys(k), yb_recv.at[ys(k)], yb_send.at[0])
+            exchange(y_buf.at[y], y_buf.at[y], sum_send.at[1], sum_recv.at[1], at(x, ys(k), z, core))
+        sized(y_buf.at[pl.ds(0, NY - 1)], sum_recv.at[1]).wait_recv()
         z_buf[z] = jnp.sum(y_buf[...], axis=0)
 
     with jax.named_scope("zsum"):
         for k in range(1, NZ):
-            exchange(z_buf, z, z_buf, z, zb_send.at[k - 1], zb_recv.at[z], at(x, y, zs(k), core))
-        for k in range(1, NZ):
-            landed(z_buf, zs(k), zb_recv.at[zs(k)], zb_send.at[0])
+            exchange(z_buf.at[z], z_buf.at[z], sum_send.at[2], sum_recv.at[2], at(x, y, zs(k), core))
+        sized(z_buf.at[pl.ds(0, NZ - 1)], sum_recv.at[2]).wait_recv()
         log_buf[core] = jnp.log(jnp.sum(z_buf[...], axis=0))
 
     with jax.named_scope("log"):
-        exchange(log_buf, core, log_buf, core, log_send.at[0], log_recv.at[core], pair)
-        landed(log_buf, 1 - core, log_recv.at[1 - core], log_send.at[0])
+        exchange(log_buf.at[core], log_buf.at[core], sum_send.at[3], sum_recv.at[3], pair)
+        sized(log_buf.at[core], sum_recv.at[3]).wait_recv()
         logs_ref[...] = log_buf[...]
 
     with jax.named_scope("drain"):
         @pl.when(fetched)
         def _():
-            for k in range(1, NH):
-                z_copy(k).wait_send()
-
-        for copy in pending:
-            copy.wait_send()
+            sized(rows.at[0, pl.ds(0, 2), core], z_send).wait_send()
+
+        @pl.when(passed_on)
+        def _():
+            sized(one_block(), z_send).wait_send()
+
+        sized(rows.at[0, pl.ds(0, NY - 1), core], y_send).wait_send()
+        sized(rows.at[pl.ds(0, 3), :, core], cross_send).wait_send()
+        sized(rows.at[:, :, core], pair_send).wait_send()
+        sized(role_buf.at[pl.ds(0, ROLES - 1)], sum_send.at[0]).wait_send()
+        sized(y_buf.at[pl.ds(0, NY - 1)], sum_send.at[1]).wait_send()
+        sized(z_buf.at[pl.ds(0, NZ - 1)], sum_send.at[2]).wait_send()
+        sized(log_buf.at[core], sum_send.at[3]).wait_send()
 
 
 def write_kernel(scaled_ref, logs_ref, center_ref, blended_ref, out_ref, blended_out, center_out, stage, sem):
@@ -327,9 +349,8 @@
             pltpu.VMEM((NH, NY, 2, rows_here, depth), jnp.bfloat16),
             pltpu.VMEM((depth, width), jnp.bfloat16),
             halves(2), halves(ROLES), halves(NY), halves(NZ), halves(2),
-            dma((4,)), dma((NH, NY, 2)), dma((NH - 1,)), dma((NY - 1,)), dma((3, NY)), dma((NH * NY,)),
-            dma((ROLES,)), dma((ROLES - 1,)), dma((NY,)), dma((NY - 1,)),
-            dma((NZ,)), dma((NZ - 1,)), dma((2,)), dma((1,)),
+            dma((4,)), pltpu.SemaphoreType.REGULAR, dma((NY,)), dma((NY,)), dma((NY,)), dma((NY,)),
+            dma, dma, dma, dma, dma((4,)), dma((4,)),
         ],
         compiler_params=pltpu.CompilerParams(collective_id=0, has_side_effects=True),
         name="gather",

time: 53.6 us -> 51.8 us (0.966)
  Pallas kernels: 52.8 us -> 51 us
    pallas_call x1, Pallas kernels: 50.9 us -> 49.1 us  [shards(): pl.pallas_call(gather_kernel, out_shape=(pltpu.VMEM((NH, NY, 2 * rows_her...]
where the time goes in v3:
time: 51.8 us; the launch traced here: 51.7 us
  Pallas kernels  51 us (98%)
  between operations  0.64 us (1%)
    pallas_call x1, Pallas kernels, shards(): pl.pallas_call(gather_kernel, out_shape=(pltpu.VMEM((NH, NY, 2 * rows_her...  49.1 us
    pallas_call x1, Pallas kernels, shards(): pl.pallas_call(write_kernel, out_shape=(jax.ShapeDtypeStruct((images, wid...  1.88 us

profile of v3, /device:TPU:1, one launch (start us, length us, event | category | flops | bytes accessed | tf_op | source)
XLA Modules:
  0.0 51.7 jit_solution(3660687114512112634)
XLA Ops:
  0.6 49.1 %gather.1 = (f32[4,8,96,256]{3,2,1,0:T(8,128)S(1)}, f32[2,1,1536]{2,1,0:T(1,128)S(1)}, f32[1,256]{1,0:T(1,128)S(1)}, f32[384,256]{1,0:T(8,128)S(1)}) custom-call(bf16[48,384]{1,0:T(8,128)(2,1)} %feat_hbm.1, f32[384,256]{1,0:T(8,128)} %tw_hbm.1, f32[384,256]{1,0:T(8,128)} %sw_hbm.1, f32[1,256]{1,0:T(1,128)} %bitcast.2), custom_call_target="tpu_custom_call" | custom-call | tf_op jit(solution)/shard_map/gather/pallas_call | solution.py:335
  49.8 1.9 %write.1 = (f32[3072,256]{1,0:T(8,128)}, f32[384,256]{1,0:T(8,128)}, f32[1,256]{1,0:T(1,128)}) custom-call(f32[4,8,96,256]{3,2,1,0:T(8,128)S(1)} %get-tuple-element.10.scaled_ref, f32[2,1,1536]{2,1,0:T(1,128)S(1)} %get-tuple-element.11.logs_ref, f32[1,256]{1,0:T(1,128)S(1)} %get-tuple-element.12.center_ref, f32[384,256]{1,0:T(8,128)S(1)} %get-tuple-element.13.blended_ref), custom_call_target="tpu_custom_call" | custom-call | tf_op jit(solution)/shard_map/write/pallas_call | solution.py:360
